TPU v7x, 32 devices: a whole 2x2x4 slice. The times are simulated.
32 devices in a mesh: row: 8 (over z, x), col: 4 (over y, core).
Axes of the slice: x: 2, y: 2, z: 4, core: 2. Of those that a mesh axis runs over, the one named last changes fastest.
Arguments:
- diag_tiles: float32 [8, 512, 512], P('row', 'col'), as said below
- sub_tiles: float32 [8, 512, 512], P('row', 'col')
- boundary: float32 [512, 512], P('col'), as said below
Outputs:
- inverse_blocks: float32 [8, 512, 512], P('row', 'col')
Inputs may be any that keep to these rules, and one draw needn't show every extreme that they name: `diag_tiles`: every tile is lower triangular, zero above the diagonal, with diagonal entries between 0.2 and 0.4. `boundary`: symmetric positive definite, smallest eigenvalue at least 2.
All inputs are finite; a program needn't handle non-finite values.
Results may differ from a plain program's by a relative error of at most 0.0003.
Values sent between devices are 32-bit elements; how exact they have to be, the bound alone decides.
A program may use at most 256 MiB of HBM per device.

v0:
```python
import jax
import jax.numpy as jnp
from jax import lax
from jax.sharding import PartitionSpec as P


def prefix(value, axis, join, neutral):
    count, mine = (lax.axis_size(axis), lax.axis_index(axis))
    pieces = jax.tree.map(lambda part: lax.all_gather(part, axis), value)
    pieces = jax.tree.map(lambda part: part[::-1], pieces)
    mine = count - 1 - mine
    so_far = jax.tree.map(
        lambda part, zero: jnp.full_like(part, 0) + jnp.asarray(zero, part.dtype), value, neutral
    )

    def hop(position, so_far):
        longer = join(so_far, jax.tree.map(lambda part: part[position], pieces))
        return jax.tree.map(lambda new, old: jnp.where(position < mine, new, old), longer, so_far)

    return lax.fori_loop(0, count - 1, hop, so_far)


def product(left, right):
    return jnp.dot(left, right, precision=lax.Precision.HIGHEST)


def advance(weight_block, inner_block, local_block):
    return local_block + product(weight_block.T, product(inner_block, weight_block))


def compose(earlier, later):
    earlier_sum, earlier_map = earlier
    later_sum, later_map = later
    return (
        later_sum + product(later_map.T, product(earlier_sum, later_map)),
        product(earlier_map, later_map),
    )


def on_device(diag_tiles, sub_tiles, boundary):
    slice_rows = diag_tiles.shape[1]
    first_row = lax.axis_index("col") * slice_rows
    inverse_all, coupling_all, end_block = (
        lax.all_gather(diag_tiles, "col", axis=1, tiled=True),
        lax.all_gather(sub_tiles, "col", axis=1, tiled=True),
        lax.all_gather(boundary, "col", axis=0, tiled=True),
    )
    blocks_here = inverse_all.shape[0]
    tile_size = inverse_all.shape[2]
    identity_map = jnp.eye(tile_size, dtype=jnp.float32)
    local_terms = jnp.einsum(
        "bki,bkj->bij", inverse_all, inverse_all, precision=lax.Precision.HIGHEST
    )
    weights = jnp.einsum("bik,bkj->bij", coupling_all, inverse_all, precision=lax.Precision.HIGHEST)
    folded_sum = local_terms[blocks_here - 1]
    folded_map = weights[blocks_here - 1]
    zero_sum = jnp.zeros((tile_size, tile_size), jnp.float32)
    entry_sum, entry_map = prefix(
        (folded_sum, folded_map), "row", compose, (zero_sum, identity_map)
    )
    current = entry_sum + product(entry_map.T, product(end_block, entry_map))
    results = [current] * blocks_here
    current = advance(weights[0], current, local_terms[0])
    results[0] = lax.dynamic_slice_in_dim(current, first_row, slice_rows, 0)
    return jnp.stack(results)


def solution(mesh):
    return jax.shard_map(
        on_device,
        mesh=mesh,
        in_specs=(P("row", "col", None), P("row", "col", None), P("col", None)),
        out_specs=P("row", "col", None),
        check_vma=False,
    )
```

profile of v0, /device:TPU:0, one launch (start us, length us, event | category | flops | bytes accessed | tf_op | source)
XLA Modules:
  0.0 421.3 jit_solution(1665118837914538444)
XLA Ops:
  6.5 0.7 all-gather.8.cloned.1.call-update
  7.3 0.7 all-gather.10.cloned.1.call-update
  8.1 20.3 %all-gather.8.cloned.1.call-done = f32[1,512,512]{2,1,0:T(8,128)} async-done(((f32[1,128,512]{2,1,0:T(8,128)}), f32[1,512,512]{2,1,0:T(8,128)}) %all-gather.8.cloned.1.call-update) | async-done | bytes 1048592 | tf_op jit(solution)/shard_map/all_gather | solution.py:44
  28.3 18.3 %all-gather.10.cloned.1.call-done = f32[1,512,512]{2,1,0:T(8,128)} async-done(((f32[1,128,512]{2,1,0:T(8,128)}), f32[1,512,512]{2,1,0:T(8,128)}) %all-gather.10.cloned.1.call-update) | async-done | bytes 1048592 | tf_op jit(solution)/shard_map/all_gather | solution.py:45
  46.6 4.4 %fusion.16 = f32[512,512]{1,0:T(8,128)} fusion(f32[1,512,512]{2,1,0:T(8,128)} %all-gather.10.cloned.1.call-done, f32[1,512,512]{2,1,0:T(8,128)} %all-gather.8.cloned.1.call-done), kind=kOutput, calls=%fused_computation.19 | convolution fusion | flops 1610612736 | bytes 3145728 | tf_op jit(solution)/shard_map/bik,bkj->bij/dot_general | solution.py:54
  51.1 0.0 all-gather.14.cloned.1.call-start
  51.2 4.5 %fusion.19 = f32[512,512]{1,0:T(8,128)} fusion(f32[1,512,512]{2,1,0:T(8,128)} %all-gather.8.cloned.1.call-done), kind=kOutput, calls=%fused_computation.22 | convolution fusion | flops 1610612736 | bytes 2097152 | tf_op jit(solution)/shard_map/bki,bkj->bij/dot_general | solution.py:51
  55.7 0.2 all-gather.12.cloned.1.call-start
  55.9 0.4 all-gather.12.cloned.1.call-update
  56.3 0.1 fusion.21
  56.4 119.3 %all-gather.16.cloned.1.call-done = f32[4096,512]{1,0:T(8,128)} async-done(((f32[512,512]{1,0:T(8,128)}), f32[4096,512]{1,0:T(8,128)}) %all-gather.16.cloned.1.call-update) | async-done | bytes 8388624 | tf_op jit(solution)/shard_map/all_gather | solution.py:9
  175.7 7.6 %rev.7 = f32[8,512,512]{2,1,0:T(8,128)} reverse(f32[8,512,512]{2,1,0:T(8,128)} %bitcast.49), dimensions={0} | reverse | bytes 16777216 | tf_op jit(solution)/shard_map/rev | solution.py:10
  183.3 117.1 %all-gather.14.cloned.1.call-done = f32[4096,512]{1,0:T(8,128)} async-done(((f32[512,512]{1,0:T(8,128)}), f32[4096,512]{1,0:T(8,128)}) %all-gather.14.cloned.1.call-update) | async-done | bytes 8388624 | tf_op jit(solution)/shard_map/all_gather | solution.py:9
  300.4 7.6 %rev.6 = f32[8,512,512]{2,1,0:T(8,128)} reverse(f32[8,512,512]{2,1,0:T(8,128)} %bitcast.50), dimensions={0} | reverse | bytes 16777216 | tf_op jit(solution)/shard_map/rev | solution.py:10
  308.0 91.8 %while.16 = (s32[]{:T(128)}, f32[512,512]{1,0:T(8,128)S(1)}, f32[512,512]{1,0:T(8,128)S(1)}, s32[]{:T(128)}, f32[8,512,512]{2,1,0:T(8,128)}, /*index=5*/f32[8,512,512]{2,1,0:T(8,128)}, s32[]{:T(128)}, s32[]{:T(128)}) while((s32[]{:T(128)}, f32[512,512]{1,0:T(8,128)S(1)}, f32[512,512]{1,0:T(8,128)S(1)}, s32[]{:T(128)}, ...), condition=%wide.region_1.2_spmd.clone, body=%wide.region_0.1_spmd.clone.sunk | while | flops 4833148928 | bytes 14682219 | solution.py:20
  308.0 4.7 %fusion.51 = f32[512,512]{1,0:T(8,128)S(1)} fusion(f32[512,512]{1,0:T(8,128)S(1)} %get-tuple-element.196, f32[8,512,512]{2,1,0:T(8,128)} %get-tuple-element.208, s32[]{:T(128)} %get-tuple-element.195, pred[]{:T(512)S(6)} %compare.3), kind=kOutput, calls=%fused_computation.6.clone.1 | convolution fusion | flops 1610874880 | bytes 3146241 | tf_op jit(solution)/shard_map/while/body/eval_jaxpr/dot_general | solution.py:24
  312.7 5.2 %fusion.52 = f32[512,512]{1,0:T(8,128)S(1)} fusion(f32[512,512]{1,0:T(8,128)S(1)} %fusion.51, f32[8,512,512]{2,1,0:T(8,128)} %get-tuple-element.207, s32[]{:T(128)} %get-tuple-element.195, f32[512,512]{1,0:T(8,128)S(1)} %get-tuple-element.196, f32[8,512,512]{2,1,0:T(8,128)} %get-tuple-element.208, pred[]{:T(512)S(6)} %compare.3, pred[]{:T(512)S(6)} %lt.27), kind=kOutput, calls=%fused_computation.3.clone.1 | convolution fusion | flops 1611399168 | bytes 5243906 | tf_op jit(solution)/shard_map/while/body/eval_jaxpr/dot_general | solution.py:24
  317.9 0.1 copy.16
  318.0 3.1 fusion.53
  321.1 4.7 %fusion.51 = f32[512,512]{1,0:T(8,128)S(1)} fusion(f32[512,512]{1,0:T(8,128)S(1)} %get-tuple-element.196, f32[8,512,512]{2,1,0:T(8,128)} %get-tuple-element.208, s32[]{:T(128)} %get-tuple-element.195, pred[]{:T(512)S(6)} %compare.3), kind=kOutput, calls=%fused_computation.6.clone.1 | convolution fusion | flops 1610874880 | bytes 3146241 | tf_op jit(solution)/shard_map/while/body/eval_jaxpr/dot_general | solution.py:24
  325.8 5.2 %fusion.52 = f32[512,512]{1,0:T(8,128)S(1)} fusion(f32[512,512]{1,0:T(8,128)S(1)} %fusion.51, f32[8,512,512]{2,1,0:T(8,128)} %get-tuple-element.207, s32[]{:T(128)} %get-tuple-element.195, f32[512,512]{1,0:T(8,128)S(1)} %get-tuple-element.196, f32[8,512,512]{2,1,0:T(8,128)} %get-tuple-element.208, pred[]{:T(512)S(6)} %compare.3, pred[]{:T(512)S(6)} %lt.27), kind=kOutput, calls=%fused_computation.3.clone.1 | convolution fusion | flops 1611399168 | bytes 5243906 | tf_op jit(solution)/shard_map/while/body/eval_jaxpr/dot_general | solution.py:24
  331.0 0.1 copy.16
  331.0 3.1 fusion.53
  334.2 4.7 %fusion.51 = f32[512,512]{1,0:T(8,128)S(1)} fusion(f32[512,512]{1,0:T(8,128)S(1)} %get-tuple-element.196, f32[8,512,512]{2,1,0:T(8,128)} %get-tuple-element.208, s32[]{:T(128)} %get-tuple-element.195, pred[]{:T(512)S(6)} %compare.3), kind=kOutput, calls=%fused_computation.6.clone.1 | convolution fusion | flops 1610874880 | bytes 3146241 | tf_op jit(solution)/shard_map/while/body/eval_jaxpr/dot_general | solution.py:24
  338.9 5.2 %fusion.52 = f32[512,512]{1,0:T(8,128)S(1)} fusion(f32[512,512]{1,0:T(8,128)S(1)} %fusion.51, f32[8,512,512]{2,1,0:T(8,128)} %get-tuple-element.207, s32[]{:T(128)} %get-tuple-element.195, f32[512,512]{1,0:T(8,128)S(1)} %get-tuple-element.196, f32[8,512,512]{2,1,0:T(8,128)} %get-tuple-element.208, pred[]{:T(512)S(6)} %compare.3, pred[]{:T(512)S(6)} %lt.27), kind=kOutput, calls=%fused_computation.3.clone.1 | convolution fusion | flops 1611399168 | bytes 5243906 | tf_op jit(solution)/shard_map/while/body/eval_jaxpr/dot_general | solution.py:24
  344.0 0.1 copy.16
  344.1 3.1 fusion.53
  347.3 4.7 %fusion.51 = f32[512,512]{1,0:T(8,128)S(1)} fusion(f32[512,512]{1,0:T(8,128)S(1)} %get-tuple-element.196, f32[8,512,512]{2,1,0:T(8,128)} %get-tuple-element.208, s32[]{:T(128)} %get-tuple-element.195, pred[]{:T(512)S(6)} %compare.3), kind=kOutput, calls=%fused_computation.6.clone.1 | convolution fusion | flops 1610874880 | bytes 3146241 | tf_op jit(solution)/shard_map/while/body/eval_jaxpr/dot_general | solution.py:24
  352.0 5.2 %fusion.52 = f32[512,512]{1,0:T(8,128)S(1)} fusion(f32[512,512]{1,0:T(8,128)S(1)} %fusion.51, f32[8,512,512]{2,1,0:T(8,128)} %get-tuple-element.207, s32[]{:T(128)} %get-tuple-element.195, f32[512,512]{1,0:T(8,128)S(1)} %get-tuple-element.196, f32[8,512,512]{2,1,0:T(8,128)} %get-tuple-element.208, pred[]{:T(512)S(6)} %compare.3, pred[]{:T(512)S(6)} %lt.27), kind=kOutput, calls=%fused_computation.3.clone.1 | convolution fusion | flops 1611399168 | bytes 5243906 | tf_op jit(solution)/shard_map/while/body/eval_jaxpr/dot_general | solution.py:24
  357.1 0.1 copy.16
  357.2 3.1 fusion.53
  360.3 4.7 %fusion.51 = f32[512,512]{1,0:T(8,128)S(1)} fusion(f32[512,512]{1,0:T(8,128)S(1)} %get-tuple-element.196, f32[8,512,512]{2,1,0:T(8,128)} %get-tuple-element.208, s32[]{:T(128)} %get-tuple-element.195, pred[]{:T(512)S(6)} %compare.3), kind=kOutput, calls=%fused_computation.6.clone.1 | convolution fusion | flops 1610874880 | bytes 3146241 | tf_op jit(solution)/shard_map/while/body/eval_jaxpr/dot_general | solution.py:24
  365.1 5.2 %fusion.52 = f32[512,512]{1,0:T(8,128)S(1)} fusion(f32[512,512]{1,0:T(8,128)S(1)} %fusion.51, f32[8,512,512]{2,1,0:T(8,128)} %get-tuple-element.207, s32[]{:T(128)} %get-tuple-element.195, f32[512,512]{1,0:T(8,128)S(1)} %get-tuple-element.196, f32[8,512,512]{2,1,0:T(8,128)} %get-tuple-element.208, pred[]{:T(512)S(6)} %compare.3, pred[]{:T(512)S(6)} %lt.27), kind=kOutput, calls=%fused_computation.3.clone.1 | convolution fusion | flops 1611399168 | bytes 5243906 | tf_op jit(solution)/shard_map/while/body/eval_jaxpr/dot_general | solution.py:24
  370.2 0.1 copy.16
  370.3 3.1 fusion.53
  373.4 4.7 %fusion.51 = f32[512,512]{1,0:T(8,128)S(1)} fusion(f32[512,512]{1,0:T(8,128)S(1)} %get-tuple-element.196, f32[8,512,512]{2,1,0:T(8,128)} %get-tuple-element.208, s32[]{:T(128)} %get-tuple-element.195, pred[]{:T(512)S(6)} %compare.3), kind=kOutput, calls=%fused_computation.6.clone.1 | convolution fusion | flops 1610874880 | bytes 3146241 | tf_op jit(solution)/shard_map/while/body/eval_jaxpr/dot_general | solution.py:24
  378.1 5.2 %fusion.52 = f32[512,512]{1,0:T(8,128)S(1)} fusion(f32[512,512]{1,0:T(8,128)S(1)} %fusion.51, f32[8,512,512]{2,1,0:T(8,128)} %get-tuple-element.207, s32[]{:T(128)} %get-tuple-element.195, f32[512,512]{1,0:T(8,128)S(1)} %get-tuple-element.196, f32[8,512,512]{2,1,0:T(8,128)} %get-tuple-element.208, pred[]{:T(512)S(6)} %compare.3, pred[]{:T(512)S(6)} %lt.27), kind=kOutput, calls=%fused_computation.3.clone.1 | convolution fusion | flops 1611399168 | bytes 5243906 | tf_op jit(solution)/shard_map/while/body/eval_jaxpr/dot_general | solution.py:24
  383.3 0.1 copy.16
  383.4 3.1 fusion.53
  386.5 4.7 %fusion.51 = f32[512,512]{1,0:T(8,128)S(1)} fusion(f32[512,512]{1,0:T(8,128)S(1)} %get-tuple-element.196, f32[8,512,512]{2,1,0:T(8,128)} %get-tuple-element.208, s32[]{:T(128)} %get-tuple-element.195, pred[]{:T(512)S(6)} %compare.3), kind=kOutput, calls=%fused_computation.6.clone.1 | convolution fusion | flops 1610874880 | bytes 3146241 | tf_op jit(solution)/shard_map/while/body/eval_jaxpr/dot_general | solution.py:24
  391.2 5.2 %fusion.52 = f32[512,512]{1,0:T(8,128)S(1)} fusion(f32[512,512]{1,0:T(8,128)S(1)} %fusion.51, f32[8,512,512]{2,1,0:T(8,128)} %get-tuple-element.207, s32[]{:T(128)} %get-tuple-element.195, f32[512,512]{1,0:T(8,128)S(1)} %get-tuple-element.196, f32[8,512,512]{2,1,0:T(8,128)} %get-tuple-element.208, pred[]{:T(512)S(6)} %compare.3, pred[]{:T(512)S(6)} %lt.27), kind=kOutput, calls=%fused_computation.3.clone.1 | convolution fusion | flops 1611399168 | bytes 5243906 | tf_op jit(solution)/shard_map/while/body/eval_jaxpr/dot_general | solution.py:24
  396.4 0.1 copy.16
  396.5 3.1 fusion.53
  399.8 4.8 %fusion.23 = f32[512,512]{1,0:T(8,128)S(1)} fusion(f32[512,512]{1,0:T(8,128)S(1)} %get-tuple-element.116, f32[512,512]{1,0:T(8,128)} %all-gather.12.cloned.1.call-done), kind=kOutput, calls=%fused_computation.28 | convolution fusion | flops 1610612736 | bytes 3145728 | tf_op jit(solution)/shard_map/dot_general | solution.py:24
  404.6 3.5 convolution_add_fusion.1
  408.1 3.1 fusion.24
  411.2 1.8 fusion.25
  413.1 1.7 fusion.22
  (9 shorter events, 0.1 us)
Async XLA Ops:
  6.5 21.8 %all-gather.8.cloned.1.call-start = ((), (), s32[]{:S(2)}) async-start(), calls=%async_computation | async-start | bytes 1310720 | tf_op jit(solution)/shard_map/all_gather | solution.py:44
  7.3 39.4 %all-gather.10.cloned.1.call-start = ((), (), s32[]{:S(2)}) async-start(), calls=%async_computation.1 | async-start | bytes 1310720 | tf_op jit(solution)/shard_map/all_gather | solution.py:45
  8.0 167.7 %all-gather.16.cloned.1.call-start = ((), (), s32[]{:S(2)}) async-start(), calls=%async_computation.4 | async-start | bytes 9437184 | tf_op jit(solution)/shard_map/all_gather | solution.py:9
  51.1 249.3 %all-gather.14.cloned.1.call-start = ((), (), s32[]{:S(2)}) async-start(), calls=%async_computation.3 | async-start | bytes 9437184 | tf_op jit(solution)/shard_map/all_gather | solution.py:9
  55.7 344.2 %all-gather.12.cloned.1.call-start = ((), (), s32[]{:S(2)}) async-start(), calls=%async_computation.2 | async-start | bytes 1310720 | tf_op jit(solution)/shard_map/all_gather | solution.py:46
  399.8 11.4 %copy-start = (f32[512,512]{1,0:T(8,128)S(1)}, f32[512,512]{1,0:T(8,128)}, u32[]{:S(2)}) copy-start(f32[512,512]{1,0:T(8,128)} %fusion.16) | copy-start | bytes 3145732
Sparse Core Ops, SparseCore 0:
  8.9 19.4 all-gather.7
  29.9 16.6 all-gather.9
  51.2 124.4 all-gather.15
  177.7 122.6 all-gather.13
  301.8 14.8 all-gather.11
where the time goes:
time: 422 us; the launch traced here: 421 us
  waiting for transfers between devices  277 us (66%)
  matrix products  113 us (27%)
  local copies, waits for them, and re-layouts  15.7 us (4%)
  between operations  13.2 us (3%)
    all_gather x2, waiting for transfers between devices, prefix(): pieces = jax.tree.map(lambda part: lax.all_gather(part, axis), value)  236 us
    dot_general x25, matrix products, product(): return jnp.dot(left, right, precision=lax.Precision.HIGHEST)  104 us
    all_gather x1, waiting for transfers between devices, on_device(): lax.all_gather(diag_tiles, 'col', axis=1, tiled=True)  20.3 us
    all_gather x1, waiting for transfers between devices, on_device(): lax.all_gather(sub_tiles, 'col', axis=1, tiled=True)  18.3 us
    rev x2, local copies, waits for them, and re-layouts, prefix(): pieces = jax.tree.map(lambda part: part[::-1], pieces)  15.2 us
  transfers between devices with their start and end apart: 5, of which 4 were waited for; matrix products, arithmetic and copies ran while one was open for 26% of the time, Pallas kernels for 0%

commit v1 on v0

v1 whole, which is shorter than its diff:
```python
import functools
import jax
import jax.numpy as jnp
from jax import lax
from jax.experimental import pallas as pl
from jax.experimental.pallas import tpu as pltpu
from jax.sharding import PartitionSpec as P

MESH = pl.DeviceIdType.MESH
F32 = jnp.float32
BF16 = jnp.bfloat16
LANES = 128


def split(x):
    high = x.astype(BF16)
    return high, (x - high.astype(F32)).astype(BF16)


def mm(a, b, transposed=False):
    (ah, al), (bh, bl) = a, b
    dims = (((1,), (1 if transposed else 0,)), ((), ()))
    dot = lambda l, r: lax.dot_general(l, r, dims, preferred_element_type=F32)
    m = ah.shape[0]
    both = dot(jnp.concatenate([ah, al], axis=0), bh)
    return both[:m] + (both[m:] + dot(ah, bl))


def kernel(rows_n, cols_n, t_in, s_in, e_in, out, t_all, s_all, zbuf, th, tl, wf, wh, wl,
           mf, mh, ml, zh, zl, sc, lo, zes, send, recv, local):
    row, c = lax.axis_index("row"), lax.axis_index("col")
    p, level = lax.rem(row, 2), row // 2
    core, y = lax.rem(c, 2), c // 2
    ny = cols_n // 2
    R, B = t_in.shape[1], t_in.shape[2]
    levels = rows_n // 2
    top = level == levels - 1
    other_y = [lax.rem(y + d, ny) for d in range(1, ny)]
    across = (row + 1 - 2 * p, c)
    partner = (row, c + 1 - 2 * core)
    beside = [(row, v * 2 + core) for v in other_y]

    barrier = pltpu.get_barrier_semaphore()
    greet = [across, partner] + beside
    for d in greet:
        pl.semaphore_signal(barrier, inc=1, device_id=d, device_id_type=MESH)

    @pl.when(level > 0)
    def _():
        pl.semaphore_signal(barrier, inc=1, device_id=(row - 2, c), device_id_type=MESH)

    @pl.when(jnp.logical_not(top))
    def _():
        pl.semaphore_signal(barrier, inc=1, device_id=(row + 2, c), device_id_type=MESH)

    above, below = levels - 1 - level, level
    peers = (above + levels - 1) // levels + (below + levels - 1) // levels
    pl.semaphore_wait(barrier, len(greet) + peers)

    bufs = (t_all, s_all, zbuf)

    def chunk(a, pp, cc, h):
        if a < 2:
            return bufs[a].at[pp, pl.ds(pl.multiple_of(cc * R + h * (R // 2), 8), R // 2), :]
        start = cc * R + pp * (R // 2) + h * (R // 4)
        return zbuf.at[pl.ds(pl.multiple_of(start, 8), R // 4), :]

    started = []
    count = [0]

    def copy(src, a, pp, cc, h, dev):
        d = pltpu.make_async_remote_copy(
            src_ref=src, dst_ref=chunk(a, pp, cc, h), send_sem=send.at[count[0]],
            recv_sem=recv.at[a, pp, cc, h], device_id=dev, device_id_type=MESH)
        count[0] += 1
        return d

    def launch(src, a, pp, cc, h, dev):
        d = copy(src, a, pp, cc, h, dev)
        d.start()
        started.append(d)

    def arrived(a, pp, cc, h):
        ref = chunk(a, pp, cc, h)
        pltpu.make_async_remote_copy(
            src_ref=ref, dst_ref=ref, send_sem=send.at[0], recv_sem=recv.at[a, pp, cc, h],
            device_id=partner, device_id_type=MESH).wait_recv()

    def own_copies(src, a):
        return [copy(src(h), a, p, c, h, d) for h in range(2) for d in [across] + beside + [partner]]

    def forward(a):
        q = 1 - p
        for h in range(2):
            arrived(a, q, c, h)
            if h == 0:
                for d in beside:
                    launch(chunk(a, q, c, h), a, q, c, h, d)
            launch(chunk(a, q, c, h), a, q, c, h, partner)
            for d in beside:
                arrived(a, p, d[1], h)
                if h == 1:
                    launch(chunk(a, p, d[1], h), a, p, d[1], h, across)
                launch(chunk(a, p, d[1], h), a, p, d[1], h, partner)

    def finish(a):
        q = 1 - p
        for h in range(2):
            for d in beside:
                arrived(a, q, d[1], h)
                launch(chunk(a, q, d[1], h), a, q, d[1], h, partner)
        for h in range(2):
            for v in [y] + other_y:
                cc = v * 2 + 1 - core
                arrived(a, p, cc, h)
                arrived(a, q, cc, h)

    for a, ref in ((0, t_in), (1, s_in)):
        for d in own_copies(lambda h: ref.at[0, pl.ds(h * (R // 2), R // 2), :], a):
            d.start()
            started.append(d)
    here = pl.ds(pl.multiple_of(c * R, 8), R)
    keep = [pltpu.make_async_copy(t_in.at[0], t_all.at[p, here, :], local.at[0]),
            pltpu.make_async_copy(s_in.at[0], s_all.at[p, here, :], local.at[1])]
    for d in keep:
        d.start()

    z_own = own_copies(lambda h: chunk(2, p, c, h), 2)
    started.extend(z_own)

    @pl.when(top)
    def _():
        mine = pltpu.make_async_copy(
            e_in.at[pl.ds(pl.multiple_of(p * (R // 2), 8), R // 2), :],
            zbuf.at[pl.ds(pl.multiple_of(c * R + p * (R // 2), 8), R // 2), :], local.at[2])
        mine.start()
        mine.wait()
        for d in z_own:
            d.start()

    for d in keep:
        d.wait()
    forward(0)
    finish(0)
    forward(1)
    for k in range(2):
        th[k], tl[k] = split(t_all[k])
    finish(1)

    def weight(i, _):
        k, at = i // (B // LANES), pl.ds(pl.multiple_of(lax.rem(i, B // LANES) * LANES, LANES), LANES)
        w = mm(split(s_all[k, at, :]), (th[k], tl[k]))
        wf[k, at, :] = w
        wh[k, at, :], wl[k, at, :] = split(w)
        return 0

    lax.fori_loop(0, 2 * (B // LANES), weight, 0)

    def joined(i, _):
        at = pl.ds(pl.multiple_of(i * LANES, LANES), LANES)
        m = mm((wh[1, at, :], wl[1, at, :]), (wh[0], wl[0]))
        mf[at, :] = m
        mh[at, :], ml[at, :] = split(m)
        return 0

    lax.fori_loop(0, B // LANES, joined, 0)

    base = pl.ds(pl.multiple_of((c * R) // LANES * LANES, LANES), LANES)
    off = lax.rem(c * R, LANES)
    turned = mm(split(wf[0, :, base].T), (th[1], tl[1]), transposed=True)
    turned = mm(split(turned), (th[1], tl[1]))
    sc[...] = mm(split(turned), (wh[0], wl[0])) + mm(split(t_all[0, :, base].T), (th[0], tl[0]))
    lo[...] = mm(split(t_all[1, :, base].T), (th[1], tl[1]))

    @pl.when(jnp.logical_not(top))
    def _():
        for h in range(2):
            arrived(2, p, c, h)
            for d in z_own[h * (len(z_own) // 2):(h + 1) * (len(z_own) // 2)]:
                d.start()

    forward(2)
    finish(2)
    zh[...], zl[...] = split(zbuf[...])
    mt = split(mf[:, base].T)
    moved = mm(mt, (zh[...], zl[...]))
    zes[...] = sc[...] + mm(split(moved), (mh[...], ml[...]))

    down = []
    for h in range(2):
        src = zes.at[pl.ds(pl.multiple_of(off + p * (R // 2) + h * (R // 4), 8), R // 4), :]
        down.append(copy(src, 2, p, c, h, (row - 2, c)))

    @pl.when(level > 0)
    def _():
        for d in down:
            d.start()

    rows = pl.ds(pl.multiple_of(off, 8), R)

    @pl.when(p == 0)
    def _():
        out[0] = zes[rows, :]

    @pl.when(p == 1)
    def _():
        step = mm(split(wf[1, :, base].T), (zh[...], zl[...]))
        lo[...] = lo[...] + mm(split(step), (wh[1], wl[1]))
        out[0] = lo[rows, :]

    for d in started:
        d.wait_send()

    @pl.when(level > 0)
    def _():
        for d in down:
            d.wait_send()


def solution(mesh):
    rows_n, cols_n = mesh.shape["row"], mesh.shape["col"]

    def on_device(t, s, e):
        R, B = t.shape[1], t.shape[2]
        ny = cols_n // 2
        sends = 3 * (2 * (ny + 1) + (ny - 1) + 2 + 5 * (ny - 1)) + 2
        vmem = pl.BlockSpec(memory_space=pltpu.VMEM)
        V = pltpu.VMEM
        return pl.pallas_call(
            functools.partial(kernel, rows_n, cols_n),
            out_shape=jax.ShapeDtypeStruct(t.shape, F32),
            in_specs=[vmem] * 3,
            out_specs=vmem,
            scratch_shapes=[
                V((2, B, B), F32), V((2, B, B), F32), V((B, B), F32),
                V((2, B, B), BF16), V((2, B, B), BF16),
                V((2, B, B), F32), V((2, B, B), BF16), V((2, B, B), BF16),
                V((B, B), F32), V((B, B), BF16), V((B, B), BF16),
                V((B, B), BF16), V((B, B), BF16),
                V((LANES, B), F32), V((LANES, B), F32), V((LANES, B), F32),
                pltpu.SemaphoreType.DMA((sends,)),
                pltpu.SemaphoreType.DMA((3, 2, cols_n, 2)),
                pltpu.SemaphoreType.DMA((3,)),
            ],
            compiler_params=pltpu.CompilerParams(collective_id=0, has_side_effects=True,
                                                 vmem_limit_bytes=56 * 2**20),
        )(t, s, e)

    return jax.shard_map(
        on_device, mesh=mesh,
        in_specs=(P("row", "col", None), P("row", "col", None), P("col", None)),
        out_specs=P("row", "col", None), check_vma=False)
```

time: 422 us -> 85.2 us (0.20)
  waiting for transfers between devices: 277 us -> 0 us
  matrix products: 113 us -> 0 us
  Pallas kernels: 0 us -> 82.4 us
  local copies, waits for them, and re-layouts: 15.7 us -> 1.67 us
  between operations: 13.2 us -> 0.01 us
    all_gather x5 -> x0, waiting for transfers between devices: 275 us -> none  [the longest x2 236 us: prefix(): pieces = jax.tree.map(lambda part: lax.all_gather(part, axis), value)]
    dot_general x27 -> x0, matrix products: 113 us -> none  [the longest x25 104 us: product(): return jnp.dot(left, right, precision=lax.Precision.HIGHEST)]
    pallas_call x0 -> x1, Pallas kernels: none -> 82.4 us  [on_device(): pl.pallas_call(functools.partial(kernel, rows_n, cols_n), out_shape=jax.S...]
    rev x2 -> x0, local copies, waits for them, and re-layouts: 15.2 us -> none  [prefix(): pieces = jax.tree.map(lambda part: part[::-1], pieces)]
  transfers between devices with their start and end apart: 5 -> 0, of which waited for: 4 -> 0; matrix products, arithmetic and copies ran while one was open for 26% -> 0% of each run, Pallas kernels for 0% -> 0%
where the time goes in v1:
time: 85.2 us; the launch traced here: 84.1 us
  Pallas kernels  82.4 us (97%)
  local copies, waits for them, and re-layouts  1.67 us (2%)
    pallas_call x1, Pallas kernels, on_device(): pl.pallas_call(functools.partial(kernel, rows_n, cols_n), out_shape=jax.S...  82.4 us

profile of v1, /device:TPU:0, one launch (start us, length us, event | category | flops | bytes accessed | tf_op | source)
XLA Modules:
  0.0 84.1 jit_solution(14292785327088191294)
XLA Ops:
  0.0 82.4 %shard_map.37 = f32[1,128,512]{2,1,0:T(8,128)} custom-call(f32[1,128,512]{2,1,0:T(8,128)} %t_in.1, f32[1,128,512]{2,1,0:T(8,128)} %s_in.1, f32[128,512]{1,0:T(8,128)} %e_in.1), custom_call_target="tpu_custom_call" | custom-call | tf_op jit(solution)/shard_map/pallas_call | solution.py:229
  82.5 1.7 %copy.5 = f32[1,128,512]{2,1,0:T(8,128)} copy(f32[1,128,512]{2,1,0:T(8,128)} %shard_map.37) | data formatting | bytes 524288

commit v2 on v1

--- a/solution.py
+++ b/solution.py
@@ -27,7 +27,7 @@
 
 
 def kernel(rows_n, cols_n, t_in, s_in, e_in, out, t_all, s_all, zbuf, th, tl, wf, wh, wl,
-           mf, mh, ml, zh, zl, sc, lo, zes, send, recv, local):
+           mf, mh, ml, zh, zl, sc, lo, zes, mbuf, sbuf, folded, send, recv, local):
     row, c = lax.axis_index("row"), lax.axis_index("col")
     p, level = lax.rem(row, 2), row // 2
     core, y = lax.rem(c, 2), c // 2
@@ -57,13 +57,17 @@
     peers = (above + levels - 1) // levels + (below + levels - 1) // levels
     pl.semaphore_wait(barrier, len(greet) + peers)
 
-    bufs = (t_all, s_all, zbuf)
+    bufs = (t_all, s_all, zbuf, mbuf, sbuf)
+    odd_level = lax.rem(level, 2) == 1
+    feeds = jnp.logical_and(odd_level, jnp.logical_not(top))
+    fed = jnp.logical_and(jnp.logical_not(odd_level), level < levels - 2)
+    sends_z = jnp.logical_and(level > 0, jnp.logical_not(feeds))
 
     def chunk(a, pp, cc, h):
         if a < 2:
             return bufs[a].at[pp, pl.ds(pl.multiple_of(cc * R + h * (R // 2), 8), R // 2), :]
         start = cc * R + pp * (R // 2) + h * (R // 4)
-        return zbuf.at[pl.ds(pl.multiple_of(start, 8), R // 4), :]
+        return bufs[a].at[pl.ds(pl.multiple_of(start, 8), R // 4), :]
 
     started = []
     count = [0]
@@ -89,7 +93,7 @@
     def own_copies(src, a):
         return [copy(src(h), a, p, c, h, d) for h in range(2) for d in [across] + beside + [partner]]
 
-    def forward(a):
+    def forward(a, between=lambda: None):
         q = 1 - p
         for h in range(2):
             arrived(a, q, c, h)
@@ -102,31 +106,62 @@
                 if h == 1:
                     launch(chunk(a, p, d[1], h), a, p, d[1], h, across)
                 launch(chunk(a, p, d[1], h), a, p, d[1], h, partner)
-
-    def finish(a):
+            if h == 0:
+                between()
+
+    def finish(a, use=lambda pp, cc: None):
         q = 1 - p
+        use(q, c)
+        for d in beside:
+            use(p, d[1])
         for h in range(2):
             for d in beside:
                 arrived(a, q, d[1], h)
                 launch(chunk(a, q, d[1], h), a, q, d[1], h, partner)
-        for h in range(2):
+        for pp in (p, q):
             for v in [y] + other_y:
-                cc = v * 2 + 1 - core
-                arrived(a, p, cc, h)
-                arrived(a, q, cc, h)
-
-    for a, ref in ((0, t_in), (1, s_in)):
-        for d in own_copies(lambda h: ref.at[0, pl.ds(h * (R // 2), R // 2), :], a):
+                for h in range(2):
+                    arrived(a, pp, v * 2 + 1 - core, h)
+                use(pp, v * 2 + 1 - core)
+        for d in beside:
+            use(q, d[1])
+
+    def start(copies):
+        for d in copies:
             d.start()
             started.append(d)
+
+    def drain():
+        for d in started:
+            d.wait_send()
+        started.clear()
+
+    t_own = own_copies(lambda h: t_in.at[0, pl.ds(h * (R // 2), R // 2), :], 0)
+    s_own = own_copies(lambda h: s_in.at[0, pl.ds(h * (R // 2), R // 2), :], 1)
+    half = len(s_own) // 2
+    start(t_own)
     here = pl.ds(pl.multiple_of(c * R, 8), R)
     keep = [pltpu.make_async_copy(t_in.at[0], t_all.at[p, here, :], local.at[0]),
             pltpu.make_async_copy(s_in.at[0], s_all.at[p, here, :], local.at[1])]
     for d in keep:
         d.start()
-
-    z_own = own_copies(lambda h: chunk(2, p, c, h), 2)
-    started.extend(z_own)
+    forward(0, lambda: start(s_own[:half]))
+    start(s_own[half:])
+    for d in keep:
+        d.wait()
+    finish(0)
+    for k in range(2):
+        th[k], tl[k] = split(t_all[k])
+
+    def weight(pp, cc):
+        at = pl.ds(pl.multiple_of(cc * R, 8), R)
+        w = mm(split(s_all[pp, at, :]), (th[pp], tl[pp]))
+        wf[pp, at, :] = w
+        wh[pp, at, :], wl[pp, at, :] = split(w)
+
+    weight(p, c)
+    forward(1)
+    first_own = own_copies(lambda h: chunk(2, p, c, h), 2)
 
     @pl.when(top)
     def _():
@@ -135,26 +170,19 @@
             zbuf.at[pl.ds(pl.multiple_of(c * R + p * (R // 2), 8), R // 2), :], local.at[2])
         mine.start()
         mine.wait()
-        for d in z_own:
+        for d in first_own:
             d.start()
 
-    for d in keep:
-        d.wait()
-    forward(0)
-    finish(0)
-    forward(1)
-    for k in range(2):
-        th[k], tl[k] = split(t_all[k])
-    finish(1)
-
-    def weight(i, _):
-        k, at = i // (B // LANES), pl.ds(pl.multiple_of(lax.rem(i, B // LANES) * LANES, LANES), LANES)
-        w = mm(split(s_all[k, at, :]), (th[k], tl[k]))
-        wf[k, at, :] = w
-        wh[k, at, :], wl[k, at, :] = split(w)
-        return 0
-
-    lax.fori_loop(0, 2 * (B // LANES), weight, 0)
+    finish(1, weight)
+    outer = list(started)
+    started.clear()
+
+    @pl.when(top)
+    def _():
+        forward(2)
+        finish(2)
+        started.extend(first_own)
+        drain()
 
     def joined(i, _):
         at = pl.ds(pl.multiple_of(i * LANES, LANES), LANES)
@@ -170,28 +198,83 @@
     turned = mm(split(wf[0, :, base].T), (th[1], tl[1]), transposed=True)
     turned = mm(split(turned), (th[1], tl[1]))
     sc[...] = mm(split(turned), (wh[0], wl[0])) + mm(split(t_all[0, :, base].T), (th[0], tl[0]))
+
+    def quarter(ref, first, h):
+        at = first + p * (R // 2) + h * (R // 4)
+        return ref.at[pl.ds(pl.multiple_of(at, 8), R // 4), :]
+
+    below_me = (row - 2, c)
+    composite = [copy(quarter(ref, first, h), a, p, c, h, below_me)
+                 for a, ref, first in ((3, mf, c * R), (4, sc, off)) for h in range(2)]
+    relay = [copy(chunk(2, p, c, h), 2, p, c, h, below_me) for h in range(2)]
+    down = [copy(quarter(zes, off, h), 2, p, c, h, below_me) for h in range(2)]
+
+    @pl.when(feeds)
+    def _():
+        for d in composite:
+            d.start()
+
     lo[...] = mm(split(t_all[1, :, base].T), (th[1], tl[1]))
 
+    @pl.when(fed)
+    def _():
+        for a in (3, 4):
+            own = own_copies(lambda h: chunk(a, p, c, h), a)
+            n = len(own) // 2
+            for h in range(2):
+                arrived(a, p, c, h)
+                start(own[h * n:(h + 1) * n])
+        for a in (3, 4):
+            forward(a)
+            finish(a)
+        drain()
+        zh[...], zl[...] = split(sbuf[...])
+        left = mm(split(mf[:, base].T), (zh[...], zl[...]))
+        sc[...] = sc[...] + mm(split(left), (mh[...], ml[...]))
+        left = mm(split(wf[1, :, base].T), (zh[...], zl[...]))
+        lo[...] = lo[...] + mm(split(left), (wh[1], wl[1]))
+
+        def fold(i, _):
+            at = pl.ds(pl.multiple_of(i * LANES, LANES), LANES)
+            m = split(mbuf[at, :])
+            folded[0, at, :] = mm(m, (mh[...], ml[...]))
+            folded[1, at, :] = mm(m, (wh[1], wl[1]))
+            return 0
+
+        lax.fori_loop(0, B // LANES, fold, 0)
+
+        def place(i, _):
+            at = pl.ds(pl.multiple_of(i * LANES, LANES), LANES)
+            mf[at, :] = folded[0, at, :]
+            mh[at, :], ml[at, :] = split(folded[0, at, :])
+            wf[1, at, :] = folded[1, at, :]
+            wh[1, at, :], wl[1, at, :] = split(folded[1, at, :])
+            return 0
+
+        lax.fori_loop(0, B // LANES, place, 0)
+
     @pl.when(jnp.logical_not(top))
     def _():
+        own = own_copies(lambda h: chunk(2, p, c, h), 2)
+        n = len(own) // 2
         for h in range(2):
             arrived(2, p, c, h)
-            for d in z_own[h * (len(z_own) // 2):(h + 1) * (len(z_own) // 2)]:
-                d.start()
-
-    forward(2)
-    finish(2)
+
+            @pl.when(feeds)
+            def _():
+                relay[h].start()
+
+            start(own[h * n:(h + 1) * n])
+        forward(2)
+        finish(2)
+        drain()
+
     zh[...], zl[...] = split(zbuf[...])
-    mt = split(mf[:, base].T)
-    moved = mm(mt, (zh[...], zl[...]))
+
+    moved = mm(split(mf[:, base].T), (zh[...], zl[...]))
     zes[...] = sc[...] + mm(split(moved), (mh[...], ml[...]))
 
-    down = []
-    for h in range(2):
-        src = zes.at[pl.ds(pl.multiple_of(off + p * (R // 2) + h * (R // 4), 8), R // 4), :]
-        down.append(copy(src, 2, p, c, h, (row - 2, c)))
-
-    @pl.when(level > 0)
+    @pl.when(sends_z)
     def _():
         for d in down:
             d.start()
@@ -208,12 +291,17 @@
         lo[...] = lo[...] + mm(split(step), (wh[1], wl[1]))
         out[0] = lo[rows, :]
 
-    for d in started:
+    for d in outer:
         d.wait_send()
 
-    @pl.when(level > 0)
+    @pl.when(sends_z)
     def _():
         for d in down:
+            d.wait_send()
+
+    @pl.when(feeds)
+    def _():
+        for d in composite + relay:
             d.wait_send()
 
 
@@ -223,7 +311,7 @@
     def on_device(t, s, e):
         R, B = t.shape[1], t.shape[2]
         ny = cols_n // 2
-        sends = 3 * (2 * (ny + 1) + (ny - 1) + 2 + 5 * (ny - 1)) + 2
+        sends = 6 * (2 * (ny + 1) + (ny - 1) + 2 + 5 * (ny - 1)) + 8
         vmem = pl.BlockSpec(memory_space=pltpu.VMEM)
         V = pltpu.VMEM
         return pl.pallas_call(
@@ -238,8 +326,9 @@
                 V((B, B), F32), V((B, B), BF16), V((B, B), BF16),
                 V((B, B), BF16), V((B, B), BF16),
                 V((LANES, B), F32), V((LANES, B), F32), V((LANES, B), F32),
+                V((B, B), F32), V((B, B), F32), V((2, B, B), F32),
                 pltpu.SemaphoreType.DMA((sends,)),
-                pltpu.SemaphoreType.DMA((3, 2, cols_n, 2)),
+                pltpu.SemaphoreType.DMA((5, 2, cols_n, 2)),
                 pltpu.SemaphoreType.DMA((3,)),
             ],
             compiler_params=pltpu.CompilerParams(collective_id=0, has_side_effects=True,

time: 85.2 us -> 73.7 us (0.87); the launches traced: 84.1 us -> 73.6 us
  Pallas kernels: 82.4 us -> 71.9 us
    pallas_call x1, Pallas kernels: 82.4 us -> 71.9 us  [on_device(): pl.pallas_call(functools.partial(kernel, rows_n, cols_n), out_shape=jax.S...]
where the time goes in v2:
time: 73.7 us; the launch traced here: 73.6 us
  Pallas kernels  71.9 us (98%)
  local copies, waits for them, and re-layouts  1.67 us (2%)
    pallas_call x1, Pallas kernels, on_device(): pl.pallas_call(functools.partial(kernel, rows_n, cols_n), out_shape=jax.S...  71.9 us
    unnamed x1, local copies, waits for them, and re-layouts  1.67 us

profile of v2, /device:TPU:0, one launch (start us, length us, event | category | flops | bytes accessed | tf_op | source)
XLA Modules:
  0.0 73.6 jit_solution(17453658902210715494)
XLA Ops:
  0.0 71.9 %shard_map.37 = f32[1,128,512]{2,1,0:T(8,128)} custom-call(f32[1,128,512]{2,1,0:T(8,128)} %t_in.1, f32[1,128,512]{2,1,0:T(8,128)} %s_in.1, f32[128,512]{1,0:T(8,128)} %e_in.1), custom_call_target="tpu_custom_call" | custom-call | tf_op jit(solution)/shard_map/pallas_call | solution.py:317
  71.9 1.7 %copy.5 = f32[1,128,512]{2,1,0:T(8,128)} copy(f32[1,128,512]{2,1,0:T(8,128)} %shard_map.37) | data formatting | bytes 524288

commit v3 on v2

--- a/solution.py
+++ b/solution.py
@@ -45,17 +45,17 @@
     for d in greet:
         pl.semaphore_signal(barrier, inc=1, device_id=d, device_id_type=MESH)
 
-    @pl.when(level > 0)
-    def _():
-        pl.semaphore_signal(barrier, inc=1, device_id=(row - 2, c), device_id_type=MESH)
-
-    @pl.when(jnp.logical_not(top))
-    def _():
-        pl.semaphore_signal(barrier, inc=1, device_id=(row + 2, c), device_id_type=MESH)
+    side = row + 1 - 2 * p
+    for step, near in ((-2, level > 0), (2, jnp.logical_not(top))):
+        @pl.when(near)
+        def _():
+            pl.semaphore_signal(barrier, inc=1, device_id=(row + step, c), device_id_type=MESH)
+            for d in beside:
+                pl.semaphore_signal(barrier, inc=1, device_id=(side + step, d[1]), device_id_type=MESH)
 
     above, below = levels - 1 - level, level
     peers = (above + levels - 1) // levels + (below + levels - 1) // levels
-    pl.semaphore_wait(barrier, len(greet) + peers)
+    pl.semaphore_wait(barrier, len(greet) + peers * (1 + len(beside)))
 
     bufs = (t_all, s_all, zbuf, mbuf, sbuf)
     odd_level = lax.rem(level, 2) == 1
@@ -63,11 +63,14 @@
     fed = jnp.logical_and(jnp.logical_not(odd_level), level < levels - 2)
     sends_z = jnp.logical_and(level > 0, jnp.logical_not(feeds))
 
+    def pieces(a):
+        return 2 if a < 2 else max(2, min(4, R // 16))
+
     def chunk(a, pp, cc, h):
         if a < 2:
             return bufs[a].at[pp, pl.ds(pl.multiple_of(cc * R + h * (R // 2), 8), R // 2), :]
-        start = cc * R + pp * (R // 2) + h * (R // 4)
-        return bufs[a].at[pl.ds(pl.multiple_of(start, 8), R // 4), :]
+        n = R // 2 // pieces(a)
+        return bufs[a].at[pl.ds(pl.multiple_of(cc * R + pp * (R // 2) + h * n, 8), n), :]
 
     started = []
     count = [0]
@@ -91,19 +94,20 @@
             device_id=partner, device_id_type=MESH).wait_recv()
 
     def own_copies(src, a):
-        return [copy(src(h), a, p, c, h, d) for h in range(2) for d in [across] + beside + [partner]]
-
-    def forward(a, between=lambda: None):
+        return [copy(src(h), a, p, c, h, d) for h in range(pieces(a))
+                for d in [across] + beside + [partner]]
+
+    def forward(a, between=lambda: None, direct=False):
         q = 1 - p
-        for h in range(2):
+        for h in range(pieces(a)):
             arrived(a, q, c, h)
-            if h == 0:
+            if h % 2 == 0 and not direct:
                 for d in beside:
                     launch(chunk(a, q, c, h), a, q, c, h, d)
             launch(chunk(a, q, c, h), a, q, c, h, partner)
             for d in beside:
                 arrived(a, p, d[1], h)
-                if h == 1:
+                if h % 2 == 1 and not direct:
                     launch(chunk(a, p, d[1], h), a, p, d[1], h, across)
                 launch(chunk(a, p, d[1], h), a, p, d[1], h, partner)
             if h == 0:
@@ -114,13 +118,13 @@
         use(q, c)
         for d in beside:
             use(p, d[1])
-        for h in range(2):
+        for h in range(pieces(a)):
             for d in beside:
                 arrived(a, q, d[1], h)
                 launch(chunk(a, q, d[1], h), a, q, d[1], h, partner)
         for pp in (p, q):
             for v in [y] + other_y:
-                for h in range(2):
+                for h in range(pieces(a)):
                     arrived(a, pp, v * 2 + 1 - core, h)
                 use(pp, v * 2 + 1 - core)
         for d in beside:
@@ -199,15 +203,18 @@
     turned = mm(split(turned), (th[1], tl[1]))
     sc[...] = mm(split(turned), (wh[0], wl[0])) + mm(split(t_all[0, :, base].T), (th[0], tl[0]))
 
-    def quarter(ref, first, h):
-        at = first + p * (R // 2) + h * (R // 4)
-        return ref.at[pl.ds(pl.multiple_of(at, 8), R // 4), :]
+    def piece(a, ref, first, h):
+        n = R // 2 // pieces(a)
+        return ref.at[pl.ds(pl.multiple_of(first + p * (R // 2) + h * n, 8), n), :]
 
     below_me = (row - 2, c)
-    composite = [copy(quarter(ref, first, h), a, p, c, h, below_me)
-                 for a, ref, first in ((3, mf, c * R), (4, sc, off)) for h in range(2)]
-    relay = [copy(chunk(2, p, c, h), 2, p, c, h, below_me) for h in range(2)]
-    down = [copy(quarter(zes, off, h), 2, p, c, h, below_me) for h in range(2)]
+    below_diagonal = [(row - 1 - 2 * p, d[1]) for d in beside]
+    composite = [copy(piece(a, ref, first, h), a, p, c, h, below_me)
+                 for a, ref, first in ((3, mf, c * R), (4, sc, off)) for h in range(pieces(a))]
+    relay = [[copy(chunk(2, p, c, h), 2, p, c, h, d) for d in [below_me] + below_diagonal]
+             for h in range(pieces(2))]
+    down = [copy(piece(2, zes, off, h), 2, p, c, h, d)
+            for d in [below_me] + below_diagonal for h in range(pieces(2))]
 
     @pl.when(feeds)
     def _():
@@ -220,8 +227,8 @@
     def _():
         for a in (3, 4):
             own = own_copies(lambda h: chunk(a, p, c, h), a)
-            n = len(own) // 2
-            for h in range(2):
+            n = len(own) // pieces(a)
+            for h in range(pieces(a)):
                 arrived(a, p, c, h)
                 start(own[h * n:(h + 1) * n])
         for a in (3, 4):
@@ -256,16 +263,23 @@
     @pl.when(jnp.logical_not(top))
     def _():
         own = own_copies(lambda h: chunk(2, p, c, h), 2)
-        n = len(own) // 2
-        for h in range(2):
+        n = len(own) // pieces(2)
+        for h in range(pieces(2)):
             arrived(2, p, c, h)
 
             @pl.when(feeds)
             def _():
-                relay[h].start()
+                relay[h][0].start()
 
             start(own[h * n:(h + 1) * n])
-        forward(2)
+
+        @pl.when(feeds)
+        def _():
+            for h in range(pieces(2)):
+                for d in relay[h][1:]:
+                    d.start()
+
+        forward(2, direct=True)
         finish(2)
         drain()
 
@@ -301,7 +315,7 @@
 
     @pl.when(feeds)
     def _():
-        for d in composite + relay:
+        for d in composite + sum(relay, []):
             d.wait_send()
 
 
@@ -311,7 +325,7 @@
     def on_device(t, s, e):
         R, B = t.shape[1], t.shape[2]
         ny = cols_n // 2
-        sends = 6 * (2 * (ny + 1) + (ny - 1) + 2 + 5 * (ny - 1)) + 8
+        sends = 12 * (2 * (ny + 1) + (ny - 1) + 2 + 5 * (ny - 1)) + 8 * (ny + 1)
         vmem = pl.BlockSpec(memory_space=pltpu.VMEM)
         V = pltpu.VMEM
         return pl.pallas_call(
@@ -328,7 +342,7 @@
                 V((LANES, B), F32), V((LANES, B), F32), V((LANES, B), F32),
                 V((B, B), F32), V((B, B), F32), V((2, B, B), F32),
                 pltpu.SemaphoreType.DMA((sends,)),
-                pltpu.SemaphoreType.DMA((5, 2, cols_n, 2)),
+                pltpu.SemaphoreType.DMA((5, 2, cols_n, 4)),
                 pltpu.SemaphoreType.DMA((3,)),
             ],
             compiler_params=pltpu.CompilerParams(collective_id=0, has_side_effects=True,

time: 73.7 us -> 70.8 us (0.961)
  Pallas kernels: 71.9 us -> 68.9 us
    pallas_call x1, Pallas kernels: 71.9 us -> 68.9 us  [on_device(): pl.pallas_call(functools.partial(kernel, rows_n, cols_n), out_shape=jax.S...]
where the time goes in v3:
time: 70.8 us; the launch traced here: 70.6 us
  Pallas kernels  68.9 us (97%)
  local copies, waits for them, and re-layouts  1.67 us (2%)
    pallas_call x1, Pallas kernels, on_device(): pl.pallas_call(functools.partial(kernel, rows_n, cols_n), out_shape=jax.S...  68.9 us
    unnamed x1, local copies, waits for them, and re-layouts  1.67 us

profile of v3, /device:TPU:0, one launch (start us, length us, event | category | flops | bytes accessed | tf_op | source)
XLA Modules:
  0.0 70.6 jit_solution(6837159395610888410)
XLA Ops:
  0.0 68.9 %shard_map.37 = f32[1,128,512]{2,1,0:T(8,128)} custom-call(f32[1,128,512]{2,1,0:T(8,128)} %t_in.1, f32[1,128,512]{2,1,0:T(8,128)} %s_in.1, f32[128,512]{1,0:T(8,128)} %e_in.1), custom_call_target="tpu_custom_call" | custom-call | tf_op jit(solution)/shard_map/pallas_call | solution.py:331
  68.9 1.7 %copy.5 = f32[1,128,512]{2,1,0:T(8,128)} copy(f32[1,128,512]{2,1,0:T(8,128)} %shard_map.37) | data formatting | bytes 524288

commit v4 on v3

--- a/solution.py
+++ b/solution.py
@@ -181,13 +181,6 @@
     outer = list(started)
     started.clear()
 
-    @pl.when(top)
-    def _():
-        forward(2)
-        finish(2)
-        started.extend(first_own)
-        drain()
-
     def joined(i, _):
         at = pl.ds(pl.multiple_of(i * LANES, LANES), LANES)
         m = mm((wh[1, at, :], wl[1, at, :]), (wh[0], wl[0]))
@@ -195,13 +188,27 @@
         mh[at, :], ml[at, :] = split(m)
         return 0
 
-    lax.fori_loop(0, B // LANES, joined, 0)
-
     base = pl.ds(pl.multiple_of((c * R) // LANES * LANES, LANES), LANES)
     off = lax.rem(c * R, LANES)
-    turned = mm(split(wf[0, :, base].T), (th[1], tl[1]), transposed=True)
-    turned = mm(split(turned), (th[1], tl[1]))
-    sc[...] = mm(split(turned), (wh[0], wl[0])) + mm(split(t_all[0, :, base].T), (th[0], tl[0]))
+
+    def sums():
+        turned = mm(split(wf[0, :, base].T), (th[1], tl[1]), transposed=True)
+        turned = mm(split(turned), (th[1], tl[1]))
+        sc[...] = mm(split(turned), (wh[0], wl[0])) + mm(split(t_all[0, :, base].T), (th[0], tl[0]))
+
+    @pl.when(top)
+    def _():
+        lax.fori_loop(0, B // LANES, joined, 0)
+        forward(2)
+        sums()
+        finish(2)
+        started.extend(first_own)
+        drain()
+
+    @pl.when(jnp.logical_not(top))
+    def _():
+        lax.fori_loop(0, B // LANES, joined, 0)
+        sums()
 
     def piece(a, ref, first, h):
         n = R // 2 // pieces(a)
@@ -221,7 +228,10 @@
         for d in composite:
             d.start()
 
-    lo[...] = mm(split(t_all[1, :, base].T), (th[1], tl[1]))
+    def odd_sum():
+        lo[...] = mm(split(t_all[1, :, base].T), (th[1], tl[1]))
+
+    pl.when(jnp.logical_not(top))(odd_sum)
 
     @pl.when(fed)
     def _():
@@ -293,6 +303,7 @@
         for d in down:
             d.start()
 
+    pl.when(top)(odd_sum)
     rows = pl.ds(pl.multiple_of(off, 8), R)
 
     @pl.when(p == 0)

time: 70.8 us -> 68.7 us (0.970)
  Pallas kernels: 68.9 us -> 66.9 us
    pallas_call x1, Pallas kernels: 68.9 us -> 66.9 us  [on_device(): pl.pallas_call(functools.partial(kernel, rows_n, cols_n), out_shape=jax.S...]
where the time goes in v4:
time: 68.7 us; the launch traced here: 68.6 us
  Pallas kernels  66.9 us (97%)
  local copies, waits for them, and re-layouts  1.67 us (2%)
    pallas_call x1, Pallas kernels, on_device(): pl.pallas_call(functools.partial(kernel, rows_n, cols_n), out_shape=jax.S...  66.9 us
    unnamed x1, local copies, waits for them, and re-layouts  1.67 us

profile of v4, /device:TPU:0, one launch (start us, length us, event | category | flops | bytes accessed | tf_op | source)
XLA Modules:
  0.0 68.6 jit_solution(17490937258634379347)
XLA Ops:
  0.0 66.9 %shard_map.37 = f32[1,128,512]{2,1,0:T(8,128)} custom-call(f32[1,128,512]{2,1,0:T(8,128)} %t_in.1, f32[1,128,512]{2,1,0:T(8,128)} %s_in.1, f32[128,512]{1,0:T(8,128)} %e_in.1), custom_call_target="tpu_custom_call" | custom-call | tf_op jit(solution)/shard_map/pallas_call | solution.py:342
  66.9 1.7 %copy.5 = f32[1,128,512]{2,1,0:T(8,128)} copy(f32[1,128,512]{2,1,0:T(8,128)} %shard_map.37) | data formatting | bytes 524288
